TPU v7x, 256 devices: a whole 4x4x8 slice. The times are simulated.
256 devices in a mesh: band: 64 (over y, z, core), feat: 4 (over x).
Axes of the slice: x: 4, y: 4, z: 8, core: 2. Of those that a mesh axis runs over, the one named last changes fastest.
Arguments:
- grid_latent: bfloat16 [131072, 512], P('band', 'feat'), may hold values from -6 to 6
- mesh_latent: bfloat16 [10240, 512], P('band', 'feat'), may hold values from -6 to 6
- edge_latent: bfloat16 [64, 4, 2048, 512], P('band', 'feat'), may hold values from -6 to 6
- edge_src: int32 [64, 8192], P('band'), may hold values from 0 to 2047
- edge_dst: int32 [64, 4, 2048], P('band', 'feat'), may hold values from 0 to 160, as said below
- edge_w1: bfloat16 [1536, 512], replicated, may hold values from -0.15625 to 0.15625
- edge_b1: float32 [512], replicated, may hold values from -3 to 3
- edge_w2: bfloat16 [512, 512], replicated, may hold values from -0.25 to 0.25
- edge_b2: float32 [512], replicated, may hold values from -2 to 2
- edge_gain: float32 [512], replicated, may hold values from 0.25 to 1.75
- edge_shift: float32 [512], replicated, may hold values from -2 to 2
- node_w1: bfloat16 [1024, 512], replicated, may hold values from -0.1875 to 0.1875
- node_b1: float32 [512], replicated, may hold values from -3 to 3
- node_w2: bfloat16 [512, 512], replicated, may hold values from -0.25 to 0.25
- node_b2: float32 [512], replicated, may hold values from -2 to 2
- node_gain: float32 [512], replicated, may hold values from 0.25 to 1.75
- node_shift: float32 [512], replicated, may hold values from -2 to 2
Outputs:
- mesh_new: bfloat16 [10240, 512], P('band', 'feat')
Inputs may be any that keep to these rules, and one draw needn't show every extreme that they name: `edge_src`: entry [s, d * 128 + j] is the grid row, counted within band index s, that sends slot j of the edges from band index s to band index d; empty slots hold some row too. `edge_dst`: entry [d, f, s * 32 + q] is the mesh node, counted within band index d, that receives slot f * 32 + q of the edges from band index s to band index d, or 160 where that slot is empty. The used slots of a pair come first; a pair has at most 128 used slots. Each receiving band index d hears only from the sending band indices of one latitude span of consecutive indices (edges are local), which lies anywhere along band since mesh partitions are face-major; other pairs are empty. In every draw some band indices receive 128 from every band index of their span.
All inputs are finite; a program needn't handle non-finite values.
Results may differ from a plain program's by a relative error of at most 0.011.
Values may be sent and summed in bfloat16 or wider, within the bound.
No kernel may reach another device: no remote copies, remote signals or barrier semaphores. Data moves between devices by JAX's collectives and lax.ppermute only.
A program may use at most 64 MiB of HBM per device.

v0:
```python
import math
import jax
import jax.numpy as jnp
from jax import lax
from jax.sharding import PartitionSpec as P

EPSILON = 1e-05


def cut_along(value, dim, length):
    shape = value.shape
    tiles = value.reshape(*shape[:dim], length, shape[dim] // length, *shape[dim + 1 :])
    return jnp.moveaxis(tiles, dim, 0)


def laid_out(tiles, dim):
    tiles = jnp.moveaxis(tiles, 0, dim)
    shape = tiles.shape
    return tiles.reshape(*shape[:dim], shape[dim] * shape[dim + 1], *shape[dim + 2 :])


def joined_exchange(value, axis, axes, splits, concats):
    sizes = [lax.axis_size(a) for a in axes]
    tiles = cut_along(value, splits[0], sizes[0])
    tiles = jnp.moveaxis(cut_along(tiles, splits[1] + 1, sizes[1]), 0, 1)
    inside = tiles.shape[2:]
    tiles = tiles.reshape(-1, *inside)
    tiles = lax.all_to_all(tiles, axis, split_axis=0, concat_axis=0, tiled=True)
    tiles = laid_out(tiles.reshape(*sizes, *inside), concats[0] + 1)
    return laid_out(tiles, concats[1])


def from_everyone(value, axis):
    length = lax.axis_size(axis)
    return lax.all_to_all(
        jnp.broadcast_to(value[None], (length, *value.shape)), axis, 0, 0, tiled=True
    )


def taken_together(value, axis):
    everything = from_everyone(value, axis)
    return jnp.sum(everything.astype(jnp.float32), axis=0)


def normalize(values, norm_gain, norm_shift):
    average = jnp.mean(values, -1, keepdims=True)
    centered = values - average
    variance = jnp.mean(centered * centered, -1, keepdims=True)
    return centered * lax.rsqrt(variance + EPSILON) * norm_gain + norm_shift


def node_step(row_block, summed, node_w1, node_b1, node_w2, node_b2, node_gain, node_shift):
    full_width = row_block.shape[1]
    hidden = jnp.dot(row_block, node_w1[:full_width], preferred_element_type=jnp.float32)
    hidden = (
        hidden
        + jnp.dot(
            summed.astype(jnp.bfloat16), node_w1[full_width:], preferred_element_type=jnp.float32
        )
        + node_b1
    )
    active = jax.nn.silu(hidden).astype(jnp.bfloat16)
    update = jnp.dot(active, node_w2, preferred_element_type=jnp.float32) + node_b2
    return (row_block.astype(jnp.float32) + normalize(update, node_gain, node_shift)).astype(
        jnp.bfloat16
    )


def select_rows(table, indices):
    total = indices.shape[0]
    block_rows = math.gcd(total, 512)
    grouped = indices.reshape(total // block_rows, block_rows)

    def one_block(block_ids):
        row_ids = lax.broadcasted_iota(jnp.int32, (block_rows, table.shape[0]), 1)
        onehot = (row_ids == block_ids[:, None]).astype(table.dtype)
        return jnp.dot(onehot, table, preferred_element_type=jnp.float32).astype(table.dtype)

    return lax.map(one_block, grouped).reshape(total, table.shape[1])


def body(
    grid_latent,
    mesh_latent,
    edge_latent,
    edge_src,
    edge_dst,
    edge_w1,
    edge_b1,
    edge_w2,
    edge_b2,
    edge_gain,
    edge_shift,
    node_w1,
    node_b1,
    node_w2,
    node_b2,
    node_gain,
    node_shift,
):
    band_count = lax.axis_size("band")
    feat_count = lax.axis_size("feat")
    quarter = grid_latent.shape[1]
    full_width = quarter * feat_count
    mesh_count = mesh_latent.shape[0]
    picked = select_rows(grid_latent, edge_src.reshape(-1)).reshape(band_count, -1, quarter)
    arrived = joined_exchange(picked, ("band", "feat"), ("band", "feat"), (0, 1), (0, 2))
    senders = arrived.reshape(-1, full_width)
    own_edges = edge_latent.reshape(-1, full_width)
    targets = edge_dst.reshape(-1)
    recv_weight = edge_w1[2 * full_width :]
    portion = lax.all_gather(mesh_latent, "feat", axis=1, tiled=True)
    projected = jnp.dot(portion, recv_weight, preferred_element_type=jnp.float32)
    node_ids = lax.broadcasted_iota(jnp.int32, (mesh_count, targets.shape[0]), 0)
    clipped = jnp.minimum(targets, mesh_count - 1)
    pick_node = (node_ids == clipped[None, :]).astype(jnp.float32)
    receiver_part = lax.dot_general(
        pick_node,
        projected,
        (((0,), (0,)), ((), ())),
        precision=lax.Precision.HIGHEST,
        preferred_element_type=jnp.float32,
    )
    hidden = jnp.dot(own_edges, edge_w1[:full_width], preferred_element_type=jnp.float32)
    hidden = hidden + jnp.dot(
        senders, edge_w1[full_width : 2 * full_width], preferred_element_type=jnp.float32
    )
    hidden = hidden + receiver_part + edge_b1
    active = jax.nn.silu(hidden).astype(jnp.bfloat16)
    update = jnp.dot(active, edge_w2, preferred_element_type=jnp.float32) + edge_b2
    edge_new = (own_edges.astype(jnp.float32) + normalize(update, edge_gain, edge_shift)).astype(
        jnp.bfloat16
    )
    selector = (node_ids == targets[None, :]).astype(jnp.bfloat16)
    partial_sums = jnp.dot(selector, edge_new, preferred_element_type=jnp.float32)
    summed = taken_together(partial_sums.astype(jnp.bfloat16), "feat").astype(jnp.float32)
    updated = node_step(portion, summed, node_w1, node_b1, node_w2, node_b2, node_gain, node_shift)
    own_cols = lax.dynamic_slice_in_dim(updated, lax.axis_index("feat") * quarter, quarter, 1)
    return own_cols


def solution(mesh):
    placed = (
        P("band", "feat"),
        P("band", "feat"),
        P("band", "feat", None, None),
        P("band", None),
        P("band", "feat", None),
        P(),
        P(),
        P(),
        P(),
        P(),
        P(),
        P(),
        P(),
        P(),
        P(),
        P(),
        P(),
    )
    return jax.shard_map(
        body, mesh=mesh, in_specs=placed, out_specs=P("band", "feat"), check_vma=False
    )
```

profile of v0, /device:TPU:1, one launch (start us, length us, event | category | flops | bytes accessed | tf_op | source)
XLA Modules:
  0.0 142.4 jit_solution(16497475571590522492)
XLA Ops:
  0.0 0.0 copy-start
  0.0 0.5 broadcast.66
  0.5 1.5 %reduce.4 = s32[8192]{0:T(1024)S(1)} reduce(s32[1,8192]{1,0:T(1,128)} %param.22, s32[]{:T(128)} %broadcast.66), dimensions={0}, to_apply=%param.22.reduce_sub_computation.3 | reduce | bytes 65540 | tf_op args[3]
  2.0 40.9 %while.10 = (s32[]{:T(128)}, bf16[16,512,128]{2,1,0:T(8,128)(2,1)}, s32[16,512]{1,0:T(8,128)S(1)}, bf16[2048,128]{1,0:T(8,128)(2,1)}, s32[]{:T(128)}) while((s32[]{:T(128)}, bf16[16,512,128]{2,1,0:T(8,128)(2,1)}, s32[16,512]{1,0:T(8,128)S(1)}, bf16[2048,128]{1,0:T(8,128)(2,1)}, s32[]{:T(128)}) %tuple.21), condition=%wide.region_1.2_spmd, body=%wide.region_0.1_spmd.sunk | while | flops 269549568 | bytes 662081 | solution.py:79
  2.0 2.5 %fusion.47 = bf16[16,512,128]{2,1,0:T(8,128)(2,1)} fusion(bf16[16,512,128]{2,1,0:T(8,128)(2,1)} %get-tuple-element.73, s32[]{:T(128)} %get-tuple-element.72, bf16[2048,128]{1,0:T(8,128)(2,1)} %get-tuple-element.80, s32[512]{0:T(512)S(1)} %bitcast.42), kind=kOutput, calls=%fused_computation.5.clone.1 | convolution fusion | flops 269549568 | bytes 657920 | tf_op jit(solution)/shard_map/while/body/eval_jaxpr/dot_general | solution.py:77
  4.6 2.5 %fusion.47 = bf16[16,512,128]{2,1,0:T(8,128)(2,1)} fusion(bf16[16,512,128]{2,1,0:T(8,128)(2,1)} %get-tuple-element.73, s32[]{:T(128)} %get-tuple-element.72, bf16[2048,128]{1,0:T(8,128)(2,1)} %get-tuple-element.80, s32[512]{0:T(512)S(1)} %bitcast.42), kind=kOutput, calls=%fused_computation.5.clone.1 | convolution fusion | flops 269549568 | bytes 657920 | tf_op jit(solution)/shard_map/while/body/eval_jaxpr/dot_general | solution.py:77
  7.1 2.5 %fusion.47 = bf16[16,512,128]{2,1,0:T(8,128)(2,1)} fusion(bf16[16,512,128]{2,1,0:T(8,128)(2,1)} %get-tuple-element.73, s32[]{:T(128)} %get-tuple-element.72, bf16[2048,128]{1,0:T(8,128)(2,1)} %get-tuple-element.80, s32[512]{0:T(512)S(1)} %bitcast.42), kind=kOutput, calls=%fused_computation.5.clone.1 | convolution fusion | flops 269549568 | bytes 657920 | tf_op jit(solution)/shard_map/while/body/eval_jaxpr/dot_general | solution.py:77
  9.7 2.6 %fusion.47 = bf16[16,512,128]{2,1,0:T(8,128)(2,1)} fusion(bf16[16,512,128]{2,1,0:T(8,128)(2,1)} %get-tuple-element.73, s32[]{:T(128)} %get-tuple-element.72, bf16[2048,128]{1,0:T(8,128)(2,1)} %get-tuple-element.80, s32[512]{0:T(512)S(1)} %bitcast.42), kind=kOutput, calls=%fused_computation.5.clone.1 | convolution fusion | flops 269549568 | bytes 657920 | tf_op jit(solution)/shard_map/while/body/eval_jaxpr/dot_general | solution.py:77
  12.3 2.5 %fusion.47 = bf16[16,512,128]{2,1,0:T(8,128)(2,1)} fusion(bf16[16,512,128]{2,1,0:T(8,128)(2,1)} %get-tuple-element.73, s32[]{:T(128)} %get-tuple-element.72, bf16[2048,128]{1,0:T(8,128)(2,1)} %get-tuple-element.80, s32[512]{0:T(512)S(1)} %bitcast.42), kind=kOutput, calls=%fused_computation.5.clone.1 | convolution fusion | flops 269549568 | bytes 657920 | tf_op jit(solution)/shard_map/while/body/eval_jaxpr/dot_general | solution.py:77
  14.8 2.5 %fusion.47 = bf16[16,512,128]{2,1,0:T(8,128)(2,1)} fusion(bf16[16,512,128]{2,1,0:T(8,128)(2,1)} %get-tuple-element.73, s32[]{:T(128)} %get-tuple-element.72, bf16[2048,128]{1,0:T(8,128)(2,1)} %get-tuple-element.80, s32[512]{0:T(512)S(1)} %bitcast.42), kind=kOutput, calls=%fused_computation.5.clone.1 | convolution fusion | flops 269549568 | bytes 657920 | tf_op jit(solution)/shard_map/while/body/eval_jaxpr/dot_general | solution.py:77
  17.4 2.5 %fusion.47 = bf16[16,512,128]{2,1,0:T(8,128)(2,1)} fusion(bf16[16,512,128]{2,1,0:T(8,128)(2,1)} %get-tuple-element.73, s32[]{:T(128)} %get-tuple-element.72, bf16[2048,128]{1,0:T(8,128)(2,1)} %get-tuple-element.80, s32[512]{0:T(512)S(1)} %bitcast.42), kind=kOutput, calls=%fused_computation.5.clone.1 | convolution fusion | flops 269549568 | bytes 657920 | tf_op jit(solution)/shard_map/while/body/eval_jaxpr/dot_general | solution.py:77
  19.9 2.5 %fusion.47 = bf16[16,512,128]{2,1,0:T(8,128)(2,1)} fusion(bf16[16,512,128]{2,1,0:T(8,128)(2,1)} %get-tuple-element.73, s32[]{:T(128)} %get-tuple-element.72, bf16[2048,128]{1,0:T(8,128)(2,1)} %get-tuple-element.80, s32[512]{0:T(512)S(1)} %bitcast.42), kind=kOutput, calls=%fused_computation.5.clone.1 | convolution fusion | flops 269549568 | bytes 657920 | tf_op jit(solution)/shard_map/while/body/eval_jaxpr/dot_general | solution.py:77
  22.5 2.5 %fusion.47 = bf16[16,512,128]{2,1,0:T(8,128)(2,1)} fusion(bf16[16,512,128]{2,1,0:T(8,128)(2,1)} %get-tuple-element.73, s32[]{:T(128)} %get-tuple-element.72, bf16[2048,128]{1,0:T(8,128)(2,1)} %get-tuple-element.80, s32[512]{0:T(512)S(1)} %bitcast.42), kind=kOutput, calls=%fused_computation.5.clone.1 | convolution fusion | flops 269549568 | bytes 657920 | tf_op jit(solution)/shard_map/while/body/eval_jaxpr/dot_general | solution.py:77
  25.0 2.5 %fusion.47 = bf16[16,512,128]{2,1,0:T(8,128)(2,1)} fusion(bf16[16,512,128]{2,1,0:T(8,128)(2,1)} %get-tuple-element.73, s32[]{:T(128)} %get-tuple-element.72, bf16[2048,128]{1,0:T(8,128)(2,1)} %get-tuple-element.80, s32[512]{0:T(512)S(1)} %bitcast.42), kind=kOutput, calls=%fused_computation.5.clone.1 | convolution fusion | flops 269549568 | bytes 657920 | tf_op jit(solution)/shard_map/while/body/eval_jaxpr/dot_general | solution.py:77
  27.6 2.5 %fusion.47 = bf16[16,512,128]{2,1,0:T(8,128)(2,1)} fusion(bf16[16,512,128]{2,1,0:T(8,128)(2,1)} %get-tuple-element.73, s32[]{:T(128)} %get-tuple-element.72, bf16[2048,128]{1,0:T(8,128)(2,1)} %get-tuple-element.80, s32[512]{0:T(512)S(1)} %bitcast.42), kind=kOutput, calls=%fused_computation.5.clone.1 | convolution fusion | flops 269549568 | bytes 657920 | tf_op jit(solution)/shard_map/while/body/eval_jaxpr/dot_general | solution.py:77
  30.1 2.5 %fusion.47 = bf16[16,512,128]{2,1,0:T(8,128)(2,1)} fusion(bf16[16,512,128]{2,1,0:T(8,128)(2,1)} %get-tuple-element.73, s32[]{:T(128)} %get-tuple-element.72, bf16[2048,128]{1,0:T(8,128)(2,1)} %get-tuple-element.80, s32[512]{0:T(512)S(1)} %bitcast.42), kind=kOutput, calls=%fused_computation.5.clone.1 | convolution fusion | flops 269549568 | bytes 657920 | tf_op jit(solution)/shard_map/while/body/eval_jaxpr/dot_general | solution.py:77
  32.7 2.5 %fusion.47 = bf16[16,512,128]{2,1,0:T(8,128)(2,1)} fusion(bf16[16,512,128]{2,1,0:T(8,128)(2,1)} %get-tuple-element.73, s32[]{:T(128)} %get-tuple-element.72, bf16[2048,128]{1,0:T(8,128)(2,1)} %get-tuple-element.80, s32[512]{0:T(512)S(1)} %bitcast.42), kind=kOutput, calls=%fused_computation.5.clone.1 | convolution fusion | flops 269549568 | bytes 657920 | tf_op jit(solution)/shard_map/while/body/eval_jaxpr/dot_general | solution.py:77
  35.2 2.5 %fusion.47 = bf16[16,512,128]{2,1,0:T(8,128)(2,1)} fusion(bf16[16,512,128]{2,1,0:T(8,128)(2,1)} %get-tuple-element.73, s32[]{:T(128)} %get-tuple-element.72, bf16[2048,128]{1,0:T(8,128)(2,1)} %get-tuple-element.80, s32[512]{0:T(512)S(1)} %bitcast.42), kind=kOutput, calls=%fused_computation.5.clone.1 | convolution fusion | flops 269549568 | bytes 657920 | tf_op jit(solution)/shard_map/while/body/eval_jaxpr/dot_general | solution.py:77
  37.8 2.5 %fusion.47 = bf16[16,512,128]{2,1,0:T(8,128)(2,1)} fusion(bf16[16,512,128]{2,1,0:T(8,128)(2,1)} %get-tuple-element.73, s32[]{:T(128)} %get-tuple-element.72, bf16[2048,128]{1,0:T(8,128)(2,1)} %get-tuple-element.80, s32[512]{0:T(512)S(1)} %bitcast.42), kind=kOutput, calls=%fused_computation.5.clone.1 | convolution fusion | flops 269549568 | bytes 657920 | tf_op jit(solution)/shard_map/while/body/eval_jaxpr/dot_general | solution.py:77
  40.3 2.5 %fusion.47 = bf16[16,512,128]{2,1,0:T(8,128)(2,1)} fusion(bf16[16,512,128]{2,1,0:T(8,128)(2,1)} %get-tuple-element.73, s32[]{:T(128)} %get-tuple-element.72, bf16[2048,128]{1,0:T(8,128)(2,1)} %get-tuple-element.80, s32[512]{0:T(512)S(1)} %bitcast.42), kind=kOutput, calls=%fused_computation.5.clone.1 | convolution fusion | flops 269549568 | bytes 657920 | tf_op jit(solution)/shard_map/while/body/eval_jaxpr/dot_general | solution.py:77
  42.9 16.6 %all-to-all-start = ((bf16[256,1,32,128]{3,2,1,0:T(8,128)(2,1)}), bf16[256,1,32,128]{3,2,1,0:T(8,128)(2,1)}, u32[]{:S(2)}, u32[]{:S(2)}) async-start(bf16[256,1,32,128]{3,2,1,0:T(8,128)(2,1)} %bitcast.4), calls=%async_computation | async-start | bytes 4194304 | tf_op jit(solution)/shard_map/all_to_all | solution.py:28
  59.5 0.0 copy-done.1
  59.5 2.5 %copy.24 = bf16[1,1,2048,512]{2,3,1,0:T(8,128)(2,1)} copy(bf16[1,1,2048,512]{3,2,1,0:T(8,128)(2,1)S(1)} %copy-done.1) | data formatting | bytes 4194304 | tf_op args[2]
  62.0 0.0 copy-done.5
  62.0 10.9 %all_gather.3 = bf16[160,512]{1,0:T(8,128)(2,1)S(1)} all-gather(bf16[160,128]{1,0:T(8,128)(2,1)S(1)} %copy-done.5), channel_id=1, replica_groups=mesh['band'=64,'feat'=4] {'feat'}, dimensions={1}, use_global_device_ids=true | all-gather | bytes 204800 | tf_op jit(solution)/shard_map/all_gather | solution.py:112
  72.9 0.0 copy-done.6
  72.9 1.3 fusion.16
  74.2 4.2 %fusion.8 = f32[2048,512]{1,0:T(8,128)} fusion(bf16[1,1,2048,512]{3,2,1,0:T(8,128)(2,1)S(1)} %copy-done.1, bf16[1536,512]{1,0:T(8,128)(2,1)} %param.24), kind=kOutput, calls=%fused_computation.14 | convolution fusion | flops 1073741824 | bytes 6815744 | tf_op jit(solution)/shard_map/dot_general | solution.py:124
  78.5 35.0 %all-to-all-done = bf16[256,1,32,128]{3,2,1,0:T(8,128)(2,1)} async-done(((bf16[256,1,32,128]{3,2,1,0:T(8,128)(2,1)}), bf16[256,1,32,128]{3,2,1,0:T(8,128)(2,1)}, u32[]{:S(2)}, u32[]{:S(2)}) %all-to-all-start) | async-done | bytes 2097184 | tf_op jit(solution)/shard_map/all_to_all | solution.py:28
  113.5 2.7 %copy.25 = bf16[64,32,4,128]{3,2,1,0:T(4,128)(2,1)S(1)} copy(bf16[64,32,4,128]{3,1,2,0:T(8,128)(2,1)} %bitcast.8) | data formatting | bytes 4194304 | tf_op jit(solution)/shard_map/transpose | solution.py:17
  116.2 0.0 copy-start.2
  116.2 0.0 copy-start.9
  116.2 2.4 %fusion.5 = f32[2048,512]{1,0:T(8,128)S(1)} fusion(bf16[256,8,4,128]{3,2,1,0:T(4,128)(2,1)S(1)} %bitcast.41, bf16[1536,512]{1,0:T(8,128)(2,1)} %param.24), kind=kOutput, calls=%fused_computation.11 | convolution fusion | flops 1073741824 | bytes 6815744 | tf_op jit(solution)/shard_map/dot_general | solution.py:125
  118.6 0.0 copy-done.2
  118.6 0.0 copy-done.9
  118.6 0.0 copy-start.7
  118.7 3.0 %multiply_convert_fusion = bf16[2048,512]{1,0:T(8,128)(2,1)S(1)} fusion(f32[2048,512]{1,0:T(8,128)S(1)} %copy-done.2, f32[2048,512]{1,0:T(8,128)S(1)} %fusion.5, f32[160,512]{1,0:T(8,128)S(1)} %fusion.16, f32[512]{0:T(512)S(1)} %copy-done.9, s32[2048]{0:T(1024)S(1)} %broadcast_minimum_fusion), kind=kOutput, calls=%fused_computation.9 | convolution fusion | flops 2021982208 | bytes 10823680 | tf_op jit(solution)/shard_map/dot_general | solution.py:117
  121.7 0.0 copy-done
  121.7 0.0 copy-done.7
  121.7 1.4 add_reduce_fusion
  123.1 0.0 copy-start.3
  123.1 0.0 copy-start.10
  123.1 0.0 copy-start.11
  123.1 0.6 multiply_reduce_fusion
  123.8 0.9 copy-done.3
  124.7 0.0 copy-done.10
  124.7 0.0 copy-done.11
  124.7 0.0 copy-start.12
  124.7 0.0 copy-start.13
  124.7 1.6 %fusion.12 = bf16[160,512]{1,0:T(8,128)(2,1)S(1)} fusion(f32[2048,512]{0,1:T(8,128)S(1)} %get-tuple-element.39, bf16[1,1,2048,512]{2,3,1,0:T(8,128)(2,1)S(1)} %copy-done.3, f32[512]{0:T(512)S(1)} %copy-done.10, f32[512]{0:T(512)S(1)} %copy-done.11, f32[2048]{0:T(1024)S(1)} %add_rsqrt_fusion, f32[2048]{0:T(1024)S(1)} %broadcast_multiply_fusion, ...), kind=kOutput, calls=%fused_computation.22 | convolution fusion | flops 344342528 | bytes 6486016 | tf_op jit(solution)/shard_map/dot_general | solution.py:135
  126.3 0.9 broadcast_in_dim.10
  127.2 3.5 %all-to-all-start.1 = ((bf16[4,160,512]{2,1,0:T(8,128)(2,1)}), bf16[4,160,512]{2,1,0:T(8,128)(2,1)S(1)}, u32[]{:S(2)}, u32[]{:S(2)}) async-start(bf16[4,160,512]{2,1,0:T(8,128)(2,1)} %broadcast_in_dim.10), calls=%async_computation.1 | async-start | bytes 1310720 | tf_op jit(solution)/shard_map/all_to_all | solution.py:35
  130.7 0.8 dynamic-slice
  131.5 0.8 dynamic-slice.1
  132.2 0.0 copy-done.4
  132.2 0.2 fusion.20
  132.5 8.3 %all-to-all-done.1 = bf16[4,160,512]{2,1,0:T(8,128)(2,1)S(1)} async-done(((bf16[4,160,512]{2,1,0:T(8,128)(2,1)}), bf16[4,160,512]{2,1,0:T(8,128)(2,1)S(1)}, u32[]{:S(2)}, u32[]{:S(2)}) %all-to-all-start.1) | async-done | bytes 655392 | tf_op jit(solution)/shard_map/all_to_all | solution.py:35
  140.8 0.1 reduce_sum.50
  140.9 0.0 copy-done.8
  140.9 0.0 copy-done.12
  140.9 0.0 copy-done.13
  140.9 0.6 fusion.33
  141.5 0.2 multiply_reduce_fusion.1
  141.7 0.7 fusion.31
  (28 shorter events, 0.1 us)
Async XLA Ops:
  0.0 121.7 %copy-start = (bf16[512,512]{1,0:T(8,128)(2,1)S(1)}, bf16[512,512]{1,0:T(8,128)(2,1)}, u32[]{:S(2)}) copy-start(bf16[512,512]{1,0:T(8,128)(2,1)} %param.26) | copy-start | bytes 1572868
  42.9 16.7 %copy-start.1 = (bf16[1,1,2048,512]{3,2,1,0:T(8,128)(2,1)S(1)}, bf16[1,1,2048,512]{3,2,1,0:T(8,128)(2,1)}, u32[]{:S(2)}) copy-start(bf16[1,1,2048,512]{3,2,1,0:T(8,128)(2,1)} %param.21) | copy-start | bytes 6291460
  42.9 19.2 %copy-start.5 = (bf16[160,128]{1,0:T(8,128)(2,1)S(1)}, bf16[160,128]{1,0:T(8,128)(2,1)}, u32[]{:S(2)}) copy-start(bf16[160,128]{1,0:T(8,128)(2,1)} %param.20) | copy-start | bytes 122884
  42.9 30.1 %copy-start.6 = (s32[1,1,2048]{2,1,0:T(1,128)S(1)}, s32[1,1,2048]{2,1,0:T(1,128)}, u32[]{:S(2)}) copy-start(s32[1,1,2048]{2,1,0:T(1,128)} %param.23) | copy-start | bytes 24580
  42.9 70.6 %all-to-all-start = ((bf16[256,1,32,128]{3,2,1,0:T(8,128)(2,1)}), bf16[256,1,32,128]{3,2,1,0:T(8,128)(2,1)}, u32[]{:S(2)}, u32[]{:S(2)}) async-start(bf16[256,1,32,128]{3,2,1,0:T(8,128)(2,1)} %bitcast.4), calls=%async_computation | async-start | bytes 4194304 | tf_op jit(solution)/shard_map/all_to_all | solution.py:28
  116.2 2.5 %copy-start.2 = (f32[2048,512]{1,0:T(8,128)S(1)}, f32[2048,512]{1,0:T(8,128)}, u32[]{:S(2)}) copy-start(f32[2048,512]{1,0:T(8,128)} %fusion.8) | copy-start | bytes 12582916
  116.2 2.5 %copy-start.9 = (f32[512]{0:T(512)S(1)}, f32[512]{0:T(512)}, u32[]{:S(2)}) copy-start(f32[512]{0:T(512)} %param.25) | copy-start | bytes 6148
  118.6 3.0 %copy-start.7 = (f32[512]{0:T(512)S(1)}, f32[512]{0:T(512)}, u32[]{:S(2)}) copy-start(f32[512]{0:T(512)} %param.27) | copy-start | bytes 6148
  123.1 1.6 %copy-start.3 = (bf16[1,1,2048,512]{2,3,1,0:T(8,128)(2,1)S(1)}, bf16[1,1,2048,512]{2,3,1,0:T(8,128)(2,1)}, u32[]{:S(2)}) copy-start(bf16[1,1,2048,512]{2,3,1,0:T(8,128)(2,1)} %copy.24) | copy-start | bytes 6291460
  123.1 1.6 %copy-start.10 = (f32[512]{0:T(512)S(1)}, f32[512]{0:T(512)}, u32[]{:S(2)}) copy-start(f32[512]{0:T(512)} %param.29) | copy-start | bytes 6148
  123.1 1.6 %copy-start.11 = (f32[512]{0:T(512)S(1)}, f32[512]{0:T(512)}, u32[]{:S(2)}) copy-start(f32[512]{0:T(512)} %param.28) | copy-start | bytes 6148
  124.7 7.6 %copy-start.4 = (bf16[1024,512]{1,0:T(8,128)(2,1)S(1)}, bf16[1024,512]{1,0:T(8,128)(2,1)}, u32[]{:S(2)}) copy-start(bf16[1024,512]{1,0:T(8,128)(2,1)} %param.30) | copy-start | bytes 3145732
  124.7 16.2 %copy-start.8 = (bf16[512,512]{1,0:T(8,128)(2,1)S(1)}, bf16[512,512]{1,0:T(8,128)(2,1)}, u32[]{:S(2)}) copy-start(bf16[512,512]{1,0:T(8,128)(2,1)} %param.32) | copy-start | bytes 1572868
  124.7 16.2 %copy-start.12 = (f32[512]{0:T(512)S(1)}, f32[512]{0:T(512)}, u32[]{:S(2)}) copy-start(f32[512]{0:T(512)} %param.33) | copy-start | bytes 6148
  124.7 16.2 %copy-start.13 = (f32[512]{0:T(512)S(1)}, f32[512]{0:T(512)}, u32[]{:S(2)}) copy-start(f32[512]{0:T(512)} %param.31) | copy-start | bytes 6148
  127.2 13.5 %all-to-all-start.1 = ((bf16[4,160,512]{2,1,0:T(8,128)(2,1)}), bf16[4,160,512]{2,1,0:T(8,128)(2,1)S(1)}, u32[]{:S(2)}, u32[]{:S(2)}) async-start(bf16[4,160,512]{2,1,0:T(8,128)(2,1)} %broadcast_in_dim.10), calls=%async_computation.1 | async-start | bytes 1310720 | tf_op jit(solution)/shard_map/all_to_all | solution.py:35
where the time goes:
time: 144 us; the launch traced here: 142 us
  matrix products  55.5 us (39%)
  waiting for transfers between devices  43.3 us (30%)
  starting transfers between devices  20.1 us (14%)
  blocking collectives  10.9 us (8%)
  local copies, waits for them, and re-layouts  9.17 us (6%)
  other arithmetic  3.13 us (2%)
    dot_general x16, matrix products, one_block(): jnp.dot(onehot, table, preferred_element_type=jnp.float32)  40.7 us
    all_to_all x1, waiting for transfers between devices, joined_exchange(): tiles = lax.all_to_all(tiles, axis, split_axis=0, concat_axis=0, tiled=True)  35 us
    all_to_all x1, starting transfers between devices, joined_exchange(): tiles = lax.all_to_all(tiles, axis, split_axis=0, concat_axis=0, tiled=True)  16.6 us
    all_gather x1, blocking collectives, body(): portion = lax.all_gather(mesh_latent, 'feat', axis=1, tiled=True)  10.9 us
    all_to_all x1, waiting for transfers between devices, from_everyone(): lax.all_to_all(jnp.broadcast_to(value[None], (length, *value.shape)), axi...  8.27 us
    dot_general x1, matrix products, body(): jnp.dot(own_edges, edge_w1[:full_width], preferred_element_type=jnp.float32)  4.24 us
    unnamed x30, local copies, waits for them, and re-layouts  3.98 us
    all_to_all x1, starting transfers between devices, from_everyone(): lax.all_to_all(jnp.broadcast_to(value[None], (length, *value.shape)), axi...  3.48 us
  transfers between devices with their start and end apart: 2, of which 2 were waited for; matrix products, arithmetic and copies ran while one was open for 7% of the time, Pallas kernels for 0%

commit v1 on v0

--- a/solution.py
+++ b/solution.py
@@ -3,6 +3,7 @@
 import jax.numpy as jnp
 from jax import lax
 from jax.sharding import PartitionSpec as P
+from jax.lax import all_to_all, axis_size
 
 EPSILON = 1e-05
 
@@ -109,7 +110,15 @@
     own_edges = edge_latent.reshape(-1, full_width)
     targets = edge_dst.reshape(-1)
     recv_weight = edge_w1[2 * full_width :]
-    portion = lax.all_gather(mesh_latent, "feat", axis=1, tiled=True)
+    portion = jnp.concatenate(
+        all_to_all(
+            jnp.stack([mesh_latent] * axis_size("feat"), 0),
+            concat_axis=0,
+            axis_name="feat",
+            split_axis=0,
+        ),
+        1,
+    )
     projected = jnp.dot(portion, recv_weight, preferred_element_type=jnp.float32)
     node_ids = lax.broadcasted_iota(jnp.int32, (mesh_count, targets.shape[0]), 0)
     clipped = jnp.minimum(targets, mesh_count - 1)

time: 144 us -> 150 us (1.042)
  waiting for transfers between devices: 43.3 us -> 54.2 us
  blocking collectives: 10.9 us -> 0 us
  starting transfers between devices: 20.1 us -> 24.9 us
  local copies, waits for them, and re-layouts: 9.17 us -> 10.8 us
    all_gather x1 -> x0, blocking collectives: 10.9 us -> none  [body(): portion = lax.all_gather(mesh_latent, 'feat', axis=1, tiled=True)]
    all_to_all x1, waiting for transfers between devices: 35 us -> 45.9 us  [joined_exchange(): tiles = lax.all_to_all(tiles, axis, split_axis=0, concat_axis=0, tiled=True)]
    all_to_all x0 -> x1, starting transfers between devices: none -> 4.83 us  [body(): all_to_all(jnp.stack([mesh_latent] * axis_size('feat'), 0), concat_axis=0...]
    another operation x0 -> x1, local copies, waits for them, and re-layouts: none -> 1.52 us  [body(): jnp.stack([mesh_latent] * axis_size('feat'), 0)]
    unnamed x30 -> x28, local copies, waits for them, and re-layouts: 3.98 us -> 4.06 us
  transfers between devices with their start and end apart: 2 -> 3, of which waited for: 2 -> 2; matrix products, arithmetic and copies ran while one was open for 7% -> 35% of each run, Pallas kernels for 0% -> 0%
where the time goes in v1:
time: 150 us; the launch traced here: 149 us
  matrix products  55.4 us (37%)
  waiting for transfers between devices  54.2 us (36%)
  starting transfers between devices  24.9 us (17%)
  local copies, waits for them, and re-layouts  10.8 us (7%)
  other arithmetic  3.14 us (2%)
    all_to_all x1, waiting for transfers between devices, joined_exchange(): tiles = lax.all_to_all(tiles, axis, split_axis=0, concat_axis=0, tiled=True)  45.9 us
    dot_general x16, matrix products, one_block(): jnp.dot(onehot, table, preferred_element_type=jnp.float32)  40.6 us
    all_to_all x1, starting transfers between devices, joined_exchange(): tiles = lax.all_to_all(tiles, axis, split_axis=0, concat_axis=0, tiled=True)  16.6 us
    all_to_all x1, waiting for transfers between devices, from_everyone(): lax.all_to_all(jnp.broadcast_to(value[None], (length, *value.shape)), axi...  8.25 us
    all_to_all x1, starting transfers between devices, body(): all_to_all(jnp.stack([mesh_latent] * axis_size('feat'), 0), concat_axis=0...  4.83 us
    dot_general x1, matrix products, body(): jnp.dot(own_edges, edge_w1[:full_width], preferred_element_type=jnp.float32)  4.22 us
    unnamed x28, local copies, waits for them, and re-layouts  4.06 us
    all_to_all x1, starting transfers between devices, from_everyone(): lax.all_to_all(jnp.broadcast_to(value[None], (length, *value.shape)), axi...  3.48 us
  transfers between devices with their start and end apart: 3, of which 2 were waited for; matrix products, arithmetic and copies ran while one was open for 35% of the time, Pallas kernels for 0%

profile of v1, /device:TPU:1, one launch (start us, length us, event | category | flops | bytes accessed | tf_op | source)
XLA Modules:
  0.0 148.7 jit_solution(6651351737301126384)
XLA Ops:
  0.0 0.0 copy-start
  0.0 1.5 %stack.2 = bf16[4,160,128]{2,1,0:T(8,128)(2,1)} broadcast(bf16[160,128]{1,0:T(8,128)(2,1)} %param.20), dimensions={1,2} | broadcast | bytes 204800 | tf_op jit(solution)/shard_map/stack | solution.py:115
  1.5 4.8 %all-to-all-start = ((bf16[4,160,128]{2,1,0:T(8,128)(2,1)}), bf16[4,160,128]{2,1,0:T(8,128)(2,1)S(1)}, u32[]{:S(2)}, u32[]{:S(2)}) async-start(bf16[4,160,128]{2,1,0:T(8,128)(2,1)} %stack.2), calls=%async_computation | async-start | bytes 327680 | tf_op jit(solution)/shard_map/all_to_all | solution.py:114
  6.4 0.6 broadcast.68
  6.9 1.5 reduce.4
  8.4 40.8 %while.10 = (s32[]{:T(128)}, bf16[16,512,128]{2,1,0:T(8,128)(2,1)}, s32[16,512]{1,0:T(8,128)S(1)}, bf16[2048,128]{1,0:T(8,128)(2,1)}, s32[]{:T(128)}) while((s32[]{:T(128)}, bf16[16,512,128]{2,1,0:T(8,128)(2,1)}, s32[16,512]{1,0:T(8,128)S(1)}, bf16[2048,128]{1,0:T(8,128)(2,1)}, s32[]{:T(128)}) %tuple.21), condition=%wide.region_1.2_spmd, body=%wide.region_0.1_spmd.sunk | while | flops 269549568 | bytes 662081 | solution.py:80
  8.4 2.5 %fusion.48 = bf16[16,512,128]{2,1,0:T(8,128)(2,1)} fusion(bf16[16,512,128]{2,1,0:T(8,128)(2,1)} %get-tuple-element.73, s32[]{:T(128)} %get-tuple-element.72, bf16[2048,128]{1,0:T(8,128)(2,1)} %get-tuple-element.80, s32[512]{0:T(512)S(1)} %bitcast.54), kind=kOutput, calls=%fused_computation.5.clone.1 | convolution fusion | flops 269549568 | bytes 657920 | tf_op jit(solution)/shard_map/while/body/eval_jaxpr/dot_general | solution.py:78
  11.0 2.5 %fusion.48 = bf16[16,512,128]{2,1,0:T(8,128)(2,1)} fusion(bf16[16,512,128]{2,1,0:T(8,128)(2,1)} %get-tuple-element.73, s32[]{:T(128)} %get-tuple-element.72, bf16[2048,128]{1,0:T(8,128)(2,1)} %get-tuple-element.80, s32[512]{0:T(512)S(1)} %bitcast.54), kind=kOutput, calls=%fused_computation.5.clone.1 | convolution fusion | flops 269549568 | bytes 657920 | tf_op jit(solution)/shard_map/while/body/eval_jaxpr/dot_general | solution.py:78
  13.5 2.5 %fusion.48 = bf16[16,512,128]{2,1,0:T(8,128)(2,1)} fusion(bf16[16,512,128]{2,1,0:T(8,128)(2,1)} %get-tuple-element.73, s32[]{:T(128)} %get-tuple-element.72, bf16[2048,128]{1,0:T(8,128)(2,1)} %get-tuple-element.80, s32[512]{0:T(512)S(1)} %bitcast.54), kind=kOutput, calls=%fused_computation.5.clone.1 | convolution fusion | flops 269549568 | bytes 657920 | tf_op jit(solution)/shard_map/while/body/eval_jaxpr/dot_general | solution.py:78
  16.1 2.5 %fusion.48 = bf16[16,512,128]{2,1,0:T(8,128)(2,1)} fusion(bf16[16,512,128]{2,1,0:T(8,128)(2,1)} %get-tuple-element.73, s32[]{:T(128)} %get-tuple-element.72, bf16[2048,128]{1,0:T(8,128)(2,1)} %get-tuple-element.80, s32[512]{0:T(512)S(1)} %bitcast.54), kind=kOutput, calls=%fused_computation.5.clone.1 | convolution fusion | flops 269549568 | bytes 657920 | tf_op jit(solution)/shard_map/while/body/eval_jaxpr/dot_general | solution.py:78
  18.6 2.5 %fusion.48 = bf16[16,512,128]{2,1,0:T(8,128)(2,1)} fusion(bf16[16,512,128]{2,1,0:T(8,128)(2,1)} %get-tuple-element.73, s32[]{:T(128)} %get-tuple-element.72, bf16[2048,128]{1,0:T(8,128)(2,1)} %get-tuple-element.80, s32[512]{0:T(512)S(1)} %bitcast.54), kind=kOutput, calls=%fused_computation.5.clone.1 | convolution fusion | flops 269549568 | bytes 657920 | tf_op jit(solution)/shard_map/while/body/eval_jaxpr/dot_general | solution.py:78
  21.2 2.5 %fusion.48 = bf16[16,512,128]{2,1,0:T(8,128)(2,1)} fusion(bf16[16,512,128]{2,1,0:T(8,128)(2,1)} %get-tuple-element.73, s32[]{:T(128)} %get-tuple-element.72, bf16[2048,128]{1,0:T(8,128)(2,1)} %get-tuple-element.80, s32[512]{0:T(512)S(1)} %bitcast.54), kind=kOutput, calls=%fused_computation.5.clone.1 | convolution fusion | flops 269549568 | bytes 657920 | tf_op jit(solution)/shard_map/while/body/eval_jaxpr/dot_general | solution.py:78
  23.7 2.5 %fusion.48 = bf16[16,512,128]{2,1,0:T(8,128)(2,1)} fusion(bf16[16,512,128]{2,1,0:T(8,128)(2,1)} %get-tuple-element.73, s32[]{:T(128)} %get-tuple-element.72, bf16[2048,128]{1,0:T(8,128)(2,1)} %get-tuple-element.80, s32[512]{0:T(512)S(1)} %bitcast.54), kind=kOutput, calls=%fused_computation.5.clone.1 | convolution fusion | flops 269549568 | bytes 657920 | tf_op jit(solution)/shard_map/while/body/eval_jaxpr/dot_general | solution.py:78
  26.3 2.5 %fusion.48 = bf16[16,512,128]{2,1,0:T(8,128)(2,1)} fusion(bf16[16,512,128]{2,1,0:T(8,128)(2,1)} %get-tuple-element.73, s32[]{:T(128)} %get-tuple-element.72, bf16[2048,128]{1,0:T(8,128)(2,1)} %get-tuple-element.80, s32[512]{0:T(512)S(1)} %bitcast.54), kind=kOutput, calls=%fused_computation.5.clone.1 | convolution fusion | flops 269549568 | bytes 657920 | tf_op jit(solution)/shard_map/while/body/eval_jaxpr/dot_general | solution.py:78
  28.8 2.5 %fusion.48 = bf16[16,512,128]{2,1,0:T(8,128)(2,1)} fusion(bf16[16,512,128]{2,1,0:T(8,128)(2,1)} %get-tuple-element.73, s32[]{:T(128)} %get-tuple-element.72, bf16[2048,128]{1,0:T(8,128)(2,1)} %get-tuple-element.80, s32[512]{0:T(512)S(1)} %bitcast.54), kind=kOutput, calls=%fused_computation.5.clone.1 | convolution fusion | flops 269549568 | bytes 657920 | tf_op jit(solution)/shard_map/while/body/eval_jaxpr/dot_general | solution.py:78
  31.4 2.5 %fusion.48 = bf16[16,512,128]{2,1,0:T(8,128)(2,1)} fusion(bf16[16,512,128]{2,1,0:T(8,128)(2,1)} %get-tuple-element.73, s32[]{:T(128)} %get-tuple-element.72, bf16[2048,128]{1,0:T(8,128)(2,1)} %get-tuple-element.80, s32[512]{0:T(512)S(1)} %bitcast.54), kind=kOutput, calls=%fused_computation.5.clone.1 | convolution fusion | flops 269549568 | bytes 657920 | tf_op jit(solution)/shard_map/while/body/eval_jaxpr/dot_general | solution.py:78
  33.9 2.5 %fusion.48 = bf16[16,512,128]{2,1,0:T(8,128)(2,1)} fusion(bf16[16,512,128]{2,1,0:T(8,128)(2,1)} %get-tuple-element.73, s32[]{:T(128)} %get-tuple-element.72, bf16[2048,128]{1,0:T(8,128)(2,1)} %get-tuple-element.80, s32[512]{0:T(512)S(1)} %bitcast.54), kind=kOutput, calls=%fused_computation.5.clone.1 | convolution fusion | flops 269549568 | bytes 657920 | tf_op jit(solution)/shard_map/while/body/eval_jaxpr/dot_general | solution.py:78
  36.5 2.5 %fusion.48 = bf16[16,512,128]{2,1,0:T(8,128)(2,1)} fusion(bf16[16,512,128]{2,1,0:T(8,128)(2,1)} %get-tuple-element.73, s32[]{:T(128)} %get-tuple-element.72, bf16[2048,128]{1,0:T(8,128)(2,1)} %get-tuple-element.80, s32[512]{0:T(512)S(1)} %bitcast.54), kind=kOutput, calls=%fused_computation.5.clone.1 | convolution fusion | flops 269549568 | bytes 657920 | tf_op jit(solution)/shard_map/while/body/eval_jaxpr/dot_general | solution.py:78
  39.0 2.5 %fusion.48 = bf16[16,512,128]{2,1,0:T(8,128)(2,1)} fusion(bf16[16,512,128]{2,1,0:T(8,128)(2,1)} %get-tuple-element.73, s32[]{:T(128)} %get-tuple-element.72, bf16[2048,128]{1,0:T(8,128)(2,1)} %get-tuple-element.80, s32[512]{0:T(512)S(1)} %bitcast.54), kind=kOutput, calls=%fused_computation.5.clone.1 | convolution fusion | flops 269549568 | bytes 657920 | tf_op jit(solution)/shard_map/while/body/eval_jaxpr/dot_general | solution.py:78
  41.6 2.5 %fusion.48 = bf16[16,512,128]{2,1,0:T(8,128)(2,1)} fusion(bf16[16,512,128]{2,1,0:T(8,128)(2,1)} %get-tuple-element.73, s32[]{:T(128)} %get-tuple-element.72, bf16[2048,128]{1,0:T(8,128)(2,1)} %get-tuple-element.80, s32[512]{0:T(512)S(1)} %bitcast.54), kind=kOutput, calls=%fused_computation.5.clone.1 | convolution fusion | flops 269549568 | bytes 657920 | tf_op jit(solution)/shard_map/while/body/eval_jaxpr/dot_general | solution.py:78
  44.1 2.5 %fusion.48 = bf16[16,512,128]{2,1,0:T(8,128)(2,1)} fusion(bf16[16,512,128]{2,1,0:T(8,128)(2,1)} %get-tuple-element.73, s32[]{:T(128)} %get-tuple-element.72, bf16[2048,128]{1,0:T(8,128)(2,1)} %get-tuple-element.80, s32[512]{0:T(512)S(1)} %bitcast.54), kind=kOutput, calls=%fused_computation.5.clone.1 | convolution fusion | flops 269549568 | bytes 657920 | tf_op jit(solution)/shard_map/while/body/eval_jaxpr/dot_general | solution.py:78
  46.6 2.5 %fusion.48 = bf16[16,512,128]{2,1,0:T(8,128)(2,1)} fusion(bf16[16,512,128]{2,1,0:T(8,128)(2,1)} %get-tuple-element.73, s32[]{:T(128)} %get-tuple-element.72, bf16[2048,128]{1,0:T(8,128)(2,1)} %get-tuple-element.80, s32[512]{0:T(512)S(1)} %bitcast.54), kind=kOutput, calls=%fused_computation.5.clone.1 | convolution fusion | flops 269549568 | bytes 657920 | tf_op jit(solution)/shard_map/while/body/eval_jaxpr/dot_general | solution.py:78
  49.2 0.0 all-to-all-done
  49.2 16.6 %all-to-all-start.1 = ((bf16[256,1,32,128]{3,2,1,0:T(8,128)(2,1)}), bf16[256,1,32,128]{3,2,1,0:T(8,128)(2,1)}, u32[]{:S(2)}, u32[]{:S(2)}) async-start(bf16[256,1,32,128]{3,2,1,0:T(8,128)(2,1)} %bitcast.5), calls=%async_computation.1 | async-start | bytes 4194304 | tf_op jit(solution)/shard_map/all_to_all | solution.py:29
  65.8 0.0 copy-done.1
  65.8 2.5 %copy.26 = bf16[1,1,2048,512]{2,3,1,0:T(8,128)(2,1)} copy(bf16[1,1,2048,512]{3,2,1,0:T(8,128)(2,1)S(1)} %copy-done.1) | data formatting | bytes 4194304 | tf_op args[2]
  68.4 0.0 copy-done.5
  68.4 4.2 %fusion.8 = f32[2048,512]{1,0:T(8,128)} fusion(bf16[1,1,2048,512]{3,2,1,0:T(8,128)(2,1)S(1)} %copy-done.1, bf16[1536,512]{1,0:T(8,128)(2,1)} %param.24), kind=kOutput, calls=%fused_computation.14 | convolution fusion | flops 1073741824 | bytes 6815744 | tf_op jit(solution)/shard_map/dot_general | solution.py:133
  72.6 1.3 fusion.16
  73.9 45.9 %all-to-all-done.1 = bf16[256,1,32,128]{3,2,1,0:T(8,128)(2,1)} async-done(((bf16[256,1,32,128]{3,2,1,0:T(8,128)(2,1)}), bf16[256,1,32,128]{3,2,1,0:T(8,128)(2,1)}, u32[]{:S(2)}, u32[]{:S(2)}) %all-to-all-start.1) | async-done | bytes 2097184 | tf_op jit(solution)/shard_map/all_to_all | solution.py:29
  119.8 2.7 %copy.27 = bf16[64,32,4,128]{3,2,1,0:T(4,128)(2,1)S(1)} copy(bf16[64,32,4,128]{3,1,2,0:T(8,128)(2,1)} %bitcast.9) | data formatting | bytes 4194304 | tf_op jit(solution)/shard_map/transpose | solution.py:18
  122.5 0.0 copy-start.2
  122.5 0.0 copy-start.8
  122.5 2.4 %fusion.5 = f32[2048,512]{1,0:T(8,128)S(1)} fusion(bf16[256,8,4,128]{3,2,1,0:T(4,128)(2,1)S(1)} %bitcast.53, bf16[1536,512]{1,0:T(8,128)(2,1)} %param.24), kind=kOutput, calls=%fused_computation.11 | convolution fusion | flops 1073741824 | bytes 6815744 | tf_op jit(solution)/shard_map/dot_general | solution.py:134
  124.9 0.0 copy-done.2
  124.9 0.0 copy-done.8
  124.9 0.0 copy-start.6
  125.0 3.0 %multiply_convert_fusion = bf16[2048,512]{1,0:T(8,128)(2,1)S(1)} fusion(f32[2048,512]{1,0:T(8,128)S(1)} %copy-done.2, f32[2048,512]{1,0:T(8,128)S(1)} %fusion.5, f32[160,512]{1,0:T(8,128)S(1)} %fusion.16, f32[512]{0:T(512)S(1)} %copy-done.8, s32[2048]{0:T(1024)S(1)} %broadcast_minimum_fusion), kind=kOutput, calls=%fused_computation.9 | convolution fusion | flops 2021982208 | bytes 10823680 | tf_op jit(solution)/shard_map/dot_general | solution.py:126
  128.0 0.0 copy-done
  128.0 0.0 copy-done.6
  128.0 1.4 add_reduce_fusion
  129.4 0.0 copy-start.3
  129.4 0.0 copy-start.9
  129.4 0.0 copy-start.10
  129.4 0.6 multiply_reduce_fusion
  130.1 0.9 copy-done.3
  131.0 0.0 copy-done.10
  131.0 1.6 %fusion.12 = bf16[160,512]{1,0:T(8,128)(2,1)S(1)} fusion(f32[2048,512]{0,1:T(8,128)S(1)} %get-tuple-element.39, bf16[1,1,2048,512]{2,3,1,0:T(8,128)(2,1)S(1)} %copy-done.3, f32[512]{0:T(512)S(1)} %copy-done.9, f32[512]{0:T(512)S(1)} %copy-done.10, f32[2048]{0:T(1024)S(1)} %add_rsqrt_fusion, f32[2048]{0:T(1024)S(1)} %broadcast_multiply_fusion, ...), kind=kOutput, calls=%fused_computation.22 | convolution fusion | flops 344342528 | bytes 6486016 | tf_op jit(solution)/shard_map/dot_general | solution.py:144
  132.6 0.0 copy-start.7
  132.6 0.0 copy-start.11
  132.6 0.0 copy-start.12
  132.6 0.9 broadcast_in_dim.10
  133.5 3.5 %all-to-all-start.2 = ((bf16[4,160,512]{2,1,0:T(8,128)(2,1)}), bf16[4,160,512]{2,1,0:T(8,128)(2,1)S(1)}, u32[]{:S(2)}, u32[]{:S(2)}) async-start(bf16[4,160,512]{2,1,0:T(8,128)(2,1)} %broadcast_in_dim.10), calls=%async_computation.2 | async-start | bytes 1310720 | tf_op jit(solution)/shard_map/all_to_all | solution.py:36
  137.0 0.8 dynamic-slice
  137.8 0.8 dynamic-slice.1
  138.6 0.2 fusion.20
  138.8 8.2 %all-to-all-done.2 = bf16[4,160,512]{2,1,0:T(8,128)(2,1)S(1)} async-done(((bf16[4,160,512]{2,1,0:T(8,128)(2,1)}), bf16[4,160,512]{2,1,0:T(8,128)(2,1)S(1)}, u32[]{:S(2)}, u32[]{:S(2)}) %all-to-all-start.2) | async-done | bytes 655392 | tf_op jit(solution)/shard_map/all_to_all | solution.py:36
  147.1 0.1 reduce_sum.50
  147.2 0.0 copy-done.7
  147.2 0.0 copy-done.11
  147.2 0.0 copy-done.12
  147.2 0.6 fusion.33
  147.8 0.2 multiply_reduce_fusion.1
  148.0 0.7 fusion.31
  (29 shorter events, 0.2 us)
Async XLA Ops:
  0.0 128.0 %copy-start = (bf16[512,512]{1,0:T(8,128)(2,1)S(1)}, bf16[512,512]{1,0:T(8,128)(2,1)}, u32[]{:S(2)}) copy-start(bf16[512,512]{1,0:T(8,128)(2,1)} %param.26) | copy-start | bytes 1572868
  1.5 47.7 %all-to-all-start = ((bf16[4,160,128]{2,1,0:T(8,128)(2,1)}), bf16[4,160,128]{2,1,0:T(8,128)(2,1)S(1)}, u32[]{:S(2)}, u32[]{:S(2)}) async-start(bf16[4,160,128]{2,1,0:T(8,128)(2,1)} %stack.2), calls=%async_computation | async-start | bytes 327680 | tf_op jit(solution)/shard_map/all_to_all | solution.py:114
  49.2 16.7 %copy-start.1 = (bf16[1,1,2048,512]{3,2,1,0:T(8,128)(2,1)S(1)}, bf16[1,1,2048,512]{3,2,1,0:T(8,128)(2,1)}, u32[]{:S(2)}) copy-start(bf16[1,1,2048,512]{3,2,1,0:T(8,128)(2,1)} %param.21) | copy-start | bytes 6291460
  49.2 19.2 %copy-start.5 = (s32[1,1,2048]{2,1,0:T(1,128)S(1)}, s32[1,1,2048]{2,1,0:T(1,128)}, u32[]{:S(2)}) copy-start(s32[1,1,2048]{2,1,0:T(1,128)} %param.23) | copy-start | bytes 24580
  49.2 70.6 %all-to-all-start.1 = ((bf16[256,1,32,128]{3,2,1,0:T(8,128)(2,1)}), bf16[256,1,32,128]{3,2,1,0:T(8,128)(2,1)}, u32[]{:S(2)}, u32[]{:S(2)}) async-start(bf16[256,1,32,128]{3,2,1,0:T(8,128)(2,1)} %bitcast.5), calls=%async_computation.1 | async-start | bytes 4194304 | tf_op jit(solution)/shard_map/all_to_all | solution.py:29
  122.5 2.5 %copy-start.2 = (f32[2048,512]{1,0:T(8,128)S(1)}, f32[2048,512]{1,0:T(8,128)}, u32[]{:S(2)}) copy-start(f32[2048,512]{1,0:T(8,128)} %fusion.8) | copy-start | bytes 12582916
  122.5 2.5 %copy-start.8 = (f32[512]{0:T(512)S(1)}, f32[512]{0:T(512)}, u32[]{:S(2)}) copy-start(f32[512]{0:T(512)} %param.25) | copy-start | bytes 6148
  124.9 3.1 %copy-start.6 = (f32[512]{0:T(512)S(1)}, f32[512]{0:T(512)}, u32[]{:S(2)}) copy-start(f32[512]{0:T(512)} %param.27) | copy-start | bytes 6148
  129.4 1.6 %copy-start.3 = (bf16[1,1,2048,512]{2,3,1,0:T(8,128)(2,1)S(1)}, bf16[1,1,2048,512]{2,3,1,0:T(8,128)(2,1)}, u32[]{:S(2)}) copy-start(bf16[1,1,2048,512]{2,3,1,0:T(8,128)(2,1)} %copy.26) | copy-start | bytes 6291460
  129.4 1.6 %copy-start.9 = (f32[512]{0:T(512)S(1)}, f32[512]{0:T(512)}, u32[]{:S(2)}) copy-start(f32[512]{0:T(512)} %param.29) | copy-start | bytes 6148
  129.4 1.6 %copy-start.10 = (f32[512]{0:T(512)S(1)}, f32[512]{0:T(512)}, u32[]{:S(2)}) copy-start(f32[512]{0:T(512)} %param.28) | copy-start | bytes 6148
  131.0 7.6 %copy-start.4 = (bf16[1024,512]{1,0:T(8,128)(2,1)S(1)}, bf16[1024,512]{1,0:T(8,128)(2,1)}, u32[]{:S(2)}) copy-start(bf16[1024,512]{1,0:T(8,128)(2,1)} %param.30) | copy-start | bytes 3145732
  132.6 14.6 %copy-start.7 = (bf16[512,512]{1,0:T(8,128)(2,1)S(1)}, bf16[512,512]{1,0:T(8,128)(2,1)}, u32[]{:S(2)}) copy-start(bf16[512,512]{1,0:T(8,128)(2,1)} %param.32) | copy-start | bytes 1572868
  132.6 14.6 %copy-start.11 = (f32[512]{0:T(512)S(1)}, f32[512]{0:T(512)}, u32[]{:S(2)}) copy-start(f32[512]{0:T(512)} %param.33) | copy-start | bytes 6148
  132.6 14.6 %copy-start.12 = (f32[512]{0:T(512)S(1)}, f32[512]{0:T(512)}, u32[]{:S(2)}) copy-start(f32[512]{0:T(512)} %param.31) | copy-start | bytes 6148
  133.5 13.5 %all-to-all-start.2 = ((bf16[4,160,512]{2,1,0:T(8,128)(2,1)}), bf16[4,160,512]{2,1,0:T(8,128)(2,1)S(1)}, u32[]{:S(2)}, u32[]{:S(2)}) async-start(bf16[4,160,512]{2,1,0:T(8,128)(2,1)} %broadcast_in_dim.10), calls=%async_computation.2 | async-start | bytes 1310720 | tf_op jit(solution)/shard_map/all_to_all | solution.py:36
